TPU v7x, 32 devices: a whole 2x2x4 slice. The times are simulated.
32 devices in a mesh: row: 4 (over z), col: 8 (over y, x, core).
Axes of the slice: x: 2, y: 2, z: 4, core: 2. Of those that a mesh axis runs over, the one named last changes fastest.
Arguments:
- matrix: float32 [15360, 15360], P('row', 'col'), may hold values from -4 to 4
- rhs: float32 [15360, 4096], P('row', 'col'), may hold values from -6 to 6
- pivot_inverses: bfloat16 [2, 512, 512], replicated, may hold values from -0.046875 to 0.046875
- panel_order: int32 [2], replicated, may hold values from 0 to 29, as said below
Outputs:
- factored: bfloat16 [15360, 15360], P('row', 'col')
- updated_rhs: float32 [15360, 4096], P('row', 'col')
- rhs_norms: float32 [4096], P('col')
Inputs may be any that keep to these rules, and one draw needn't show every extreme that they name: `panel_order`: two different panel indices, one of which is the last panel, 29.
All inputs are finite; a program needn't handle non-finite values.
Results may differ from a plain program's by a relative error of at most 0.001.
Values sent between devices are 32-bit elements; how exact they have to be, the bound alone decides.
No kernel may reach another device: no remote copies, remote signals or barrier semaphores. Data moves between devices by JAX's collectives and lax.ppermute only.
A program may use at most 192 MiB of HBM per device.

v0:
```python
import jax
import jax.numpy as jnp
from jax import lax
from jax.sharding import PartitionSpec as P

N = 15360
PW = 512


def product(first, second):
    return jnp.dot(
        first, second, precision=lax.Precision.HIGHEST, preferred_element_type=jnp.float32
    )


def cut_along(values, start, length, axis_dim):
    return lax.dynamic_slice_in_dim(values, start, length, axis_dim)


def refresh(sub_block, mult_rows, upper_rows, row_keep, col_keep, fresh_col, placed):
    updated = sub_block - row_keep[:, None] * product(mult_rows, upper_rows * col_keep[None, :])
    return jnp.where((row_keep[:, None] > 0) & (fresh_col[None, :] > 0), placed, updated)


def on_device(matrix, rhs, pivot_inverses, panel_order):
    row_count = lax.axis_size("row")
    col_count = lax.axis_size("col")
    block_size = PW // row_count
    group_count = col_count // row_count
    col_index = lax.axis_index("col")
    row_len, col_len = matrix.shape
    row_block_id = jnp.arange(row_len, dtype=jnp.int32) // block_size
    col_block_id = jnp.arange(col_len, dtype=jnp.int32) // block_size

    def column_hit(panel_id):
        is_owner = col_index // row_count == panel_id % group_count
        return (
            ((col_block_id == panel_id // group_count) & is_owner).astype(jnp.float32),
            is_owner,
        )

    def take_slices(current, right_sides, panel_id):
        start = panel_id * block_size
        return (
            cut_along(current, start, block_size, 0),
            cut_along(right_sides, start, block_size, 0),
            cut_along(current, panel_id // group_count * block_size, block_size, 1),
        )

    current = matrix
    right_sides = rhs
    row_piece, rhs_piece, column_slab = take_slices(current, right_sides, panel_order[0])
    for section in range(2):
        panel_id = panel_order[section]
        row_keep = jnp.ones((row_len,), jnp.float32)
        col_keep = jnp.ones((col_len,), jnp.float32)
        for earlier in range(section + 1):
            row_keep = row_keep * (row_block_id != panel_order[earlier]).astype(jnp.float32)
            hit, owner_flag = column_hit(panel_order[earlier])
            col_keep = col_keep * (1.0 - hit)
        fresh_col, keep_is_owner = column_hit(panel_order[section])
        row_keep, col_keep, fresh_col, is_owner = (row_keep, col_keep, fresh_col, keep_is_owner)
        upper_rows, rhs_rows = (
            lax.all_gather(row_piece, "row", axis=0, tiled=True),
            lax.all_gather(rhs_piece, "row", axis=0, tiled=True),
        )
        inverse = pivot_inverses[section].astype(jnp.float32)
        own_rows = cut_along(inverse, col_index % row_count * block_size, block_size, 0)
        partial_value = jnp.where(is_owner, product(column_slab, own_rows), 0.0)
        multipliers = lax.psum(partial_value, "col")
        own_mult = cut_along(multipliers, col_index % row_count * block_size, block_size, 1)
        placed = lax.dynamic_update_slice_in_dim(
            jnp.zeros_like(current), own_mult, panel_id // group_count * block_size, 1
        )
        current = refresh(current, multipliers, upper_rows, row_keep, col_keep, fresh_col, placed)
        right_sides = right_sides - row_keep[:, None] * product(multipliers, rhs_rows)
        if section == 0:
            row_piece, rhs_piece, column_slab = take_slices(current, right_sides, panel_order[1])
    totals = lax.psum(jnp.sum(right_sides * right_sides, axis=0), "row")
    rhs_norms = jnp.sqrt(totals / N + 1e-06)
    return (current.astype(jnp.bfloat16), right_sides, rhs_norms)


def solution(mesh):
    in_specs = (P("row", "col"), P("row", "col"), P(), P())
    out_specs = (P("row", "col"), P("row", "col"), P("col"))
    return jax.shard_map(
        on_device, mesh=mesh, in_specs=in_specs, out_specs=out_specs, check_vma=False
    )
```

profile of v0, /device:TPU:0, one launch (start us, length us, event | category | flops | bytes accessed | tf_op | source)
XLA Modules:
  0.0 484.2 jit_solution(17791880367086263619)
XLA Ops:
  8.0 0.0 all-gather.9.cloned.1.call-start
  8.0 1.4 fusion.28
  10.1 1.7 constant_dynamic-slice_fusion.3
  11.8 0.0 all-reduce.3.cloned.1.call-start
  14.5 1.3 fusion.27
  15.7 6.9 %convolution_select_fusion.1 = f32[3840,512]{1,0:T(8,128)} fusion(pred[]{:T(512)S(6)} %eq.59, f32[3840,1920]{1,0:T(8,128)} %param.4, s32[]{:T(128)S(6)} %select_n.140, bf16[1,512,512]{2,1,0:T(8,128)(2,1)S(1)} %get-tuple-element.4, s32[]{:T(128)S(6)} %select_n.142), kind=kOutput, calls=%fused_computation.6 | convolution fusion | flops 3021864960 | bytes 9961481 | tf_op jit(solution)/shard_map/dot_general | solution.py:11
  22.7 0.0 all-gather.5.cloned.1.call-start
  22.7 2.3 constant_dynamic-slice_fusion.2
  25.0 0.0 all-gather.11.cloned.1.call-start
  28.5 0.7 broadcast_compare_fusion
  29.2 0.7 fusion.15
  29.9 12.8 %all-gather.9.cloned.1.call-done = f32[512,512]{1,0:T(8,128)} async-done(((f32[128,512]{1,0:T(8,128)}), f32[512,512]{1,0:T(8,128)}) %all-gather.9.cloned.1.call-update) | async-done | bytes 1048592 | tf_op jit(solution)/shard_map/all_gather | solution.py:65
  42.6 103.8 %all-reduce.3.cloned.1.call-done = f32[3840,512]{1,0:T(8,128)} async-done(((f32[3840,512]{1,0:T(8,128)}), f32[3840,512]{1,0:T(8,128)}) %all-reduce.3.cloned.1.call-update) | async-done | bytes 7864336 | tf_op jit(solution)/shard_map/psum | solution.py:70
  146.4 16.6 %multiply_subtract_fusion.1 = f32[3840,512]{1,0:T(8,128)S(1)} fusion(f32[3840,512]{1,0:T(8,128)} %param.5, f32[3840,512]{1,0:T(8,128)} %all-reduce.3.cloned.1.call-done, f32[512,512]{1,0:T(8,128)} %all-gather.9.cloned.1.call-done, f32[3840]{0:T(1024)S(1)} %fusion.15), kind=kOutput, calls=%fused_computation.4 | convolution fusion | flops 12083527680 | bytes 24656896 | tf_op jit(solution)/shard_map/dot_general | solution.py:11
  163.0 3.2 copy-done
  166.2 0.7 constant_dynamic-slice_fusion
  167.0 0.2 all-reduce.5.cloned.1.call-start
  167.2 11.9 %broadcast.286.clone = f32[3840,1920]{1,0:T(8,128)} broadcast(f32[]{:T(128)} %constant.140.clone.1), dimensions={} | broadcast | bytes 29491204 | tf_op jit(solution)/shard_map/broadcast.6
  179.1 3.1 dynamic-slice_dynamic-update-slice_fusion.1
  182.2 61.2 %subtract_select_fusion = f32[3840,1920]{1,0:T(8,128)} fusion(f32[3840,1920]{1,0:T(8,128)} %dynamic-slice_dynamic-update-slice_fusion.1, f32[3840,1920]{1,0:T(8,128)} %param.4, f32[3840,512]{1,0:T(8,128)} %all-reduce.3.cloned.1.call-done, f32[3840]{0:T(1024)S(1)} %fusion.15, pred[1920]{0:T(1024)(128)(4,1)S(1)} %convert_compare_fusion, ...), kind=kOutput, calls=%fused_computation.1 | convolution fusion | flops 45328957440 | bytes 100298880 | tf_op jit(solution)/shard_map/dot_general | solution.py:11
  243.4 6.9 %convolution_select_fusion = f32[3840,512]{1,0:T(8,128)} fusion(pred[]{:T(512)S(6)} %eq.56, f32[3840,1920]{1,0:T(8,128)} %subtract_select_fusion, s32[]{:T(128)S(6)} %select_n.146, bf16[1,512,512]{2,1,0:T(8,128)(2,1)S(1)} %get-tuple-element.3, s32[]{:T(128)S(6)} %select_n.142), kind=kOutput, calls=%fused_computation.5 | convolution fusion | flops 3021864960 | bytes 9961481 | tf_op jit(solution)/shard_map/dot_general | solution.py:11
  250.3 0.3 all-gather.7.cloned.1.call-start
  250.6 2.2 constant_dynamic-slice_fusion.1
  252.8 1.3 broadcast_compare_fusion.1
  254.2 1.3 fusion.14
  255.6 115.9 %all-reduce.5.cloned.1.call-done = f32[3840,512]{1,0:T(8,128)} async-done(((f32[3840,512]{1,0:T(8,128)}), f32[3840,512]{1,0:T(8,128)}) %all-reduce.5.cloned.1.call-update) | async-done | bytes 7864336 | tf_op jit(solution)/shard_map/psum | solution.py:70
  371.5 17.8 %multiply_reduce_fusion = (f32[512]{0:T(512)S(1)}, f32[3840,512]{1,0:T(8,128)}) fusion(f32[3840,512]{1,0:T(8,128)} %copy-done, f32[3840,512]{1,0:T(8,128)} %all-reduce.5.cloned.1.call-done, f32[512,512]{1,0:T(8,128)} %all-gather.11.cloned.1.call-done, f32[3840]{0:T(1024)S(1)} %fusion.14), kind=kOutput, calls=%fused_computation.2 | convolution fusion | flops 12087459840 | bytes 24658944 | tf_op jit(solution)/shard_map/dot_general | solution.py:11
  389.2 11.7 %psum.23 = f32[512]{0:T(512)S(1)} all-reduce(f32[512]{0:T(512)S(1)} %get-tuple-element.7), channel_id=1, replica_groups=mesh['row'=4,'col'=8] {'row'}, use_global_device_ids=true, to_apply=%region_3.4 | all-reduce | flops 512 | bytes 4096 | tf_op jit(solution)/shard_map/psum | solution.py:79
  400.9 0.6 add_sqrt_fusion
  401.5 11.6 %broadcast.286 = f32[3840,1920]{1,0:T(8,128)} broadcast(f32[]{:T(128)} %constant.140.clone.1), dimensions={} | broadcast | bytes 29491204 | tf_op jit(solution)/shard_map/broadcast.6
  413.1 3.1 dynamic-slice_dynamic-update-slice_fusion
  416.2 60.9 %select_convert_fusion = bf16[3840,1920]{1,0:T(8,128)(2,1)} fusion(f32[3840,1920]{1,0:T(8,128)} %dynamic-slice_dynamic-update-slice_fusion, f32[3840,1920]{1,0:T(8,128)} %subtract_select_fusion, f32[3840,512]{1,0:T(8,128)} %all-reduce.5.cloned.1.call-done, f32[3840]{0:T(1024)S(1)} %fusion.14, pred[1920]{0:T(1024)(128)(4,1)S(1)} %convert_compare_fusion.1, ...), kind=kOutput, calls=%fused_computation | convolution fusion | flops 45328957440 | bytes 85553280 | tf_op jit(solution)/shard_map/dot_general | solution.py:11
  (14 shorter events, 0.2 us)
Async XLA Ops:
  8.0 34.6 %all-gather.9.cloned.1.call-start = ((), (), s32[]{:S(2)}) async-start(), calls=%async_computation.4 | async-start | bytes 1310720 | tf_op jit(solution)/shard_map/all_gather | solution.py:65
  11.8 134.6 %all-reduce.3.cloned.1.call-start = ((), (), s32[]{:S(2)}) async-start(), calls=%async_computation | async-start | bytes 15728640 | tf_op jit(solution)/shard_map/psum | solution.py:70
  22.7 159.6 %all-gather.5.cloned.1.call-start = ((), (), s32[]{:S(2)}) async-start(), calls=%async_computation.1 | async-start | bytes 4915200 | tf_op jit(solution)/shard_map/all_gather | solution.py:64
  25.0 230.5 %all-gather.11.cloned.1.call-start = ((), (), s32[]{:S(2)}) async-start(), calls=%async_computation.5 | async-start | bytes 1310720 | tf_op jit(solution)/shard_map/all_gather | solution.py:65
  163.0 3.2 copy-start
  167.0 204.5 %all-reduce.5.cloned.1.call-start = ((), (), s32[]{:S(2)}) async-start(), calls=%async_computation.2 | async-start | bytes 15728640 | tf_op jit(solution)/shard_map/psum | solution.py:70
  250.3 165.9 %all-gather.7.cloned.1.call-start = ((), (), s32[]{:S(2)}) async-start(), calls=%async_computation.3 | async-start | bytes 4915200 | tf_op jit(solution)/shard_map/all_gather | solution.py:64
Sparse Core Ops, SparseCore 0:
  11.9 30.6 all-gather.8
  44.2 75.7 all-gather.4
  167.1 28.0 all-gather.10
  252.9 76.5 all-gather.6
Sparse Core Ops, SparseCore 1:
  22.7 123.6 all-reduce.2
  250.4 121.0 all-reduce.4
where the time goes:
time: 485 us; the launch traced here: 484 us
  waiting for transfers between devices  233 us (48%)
  matrix products  170 us (35%)
  local copies, waits for them, and re-layouts  42.5 us (9%)
  between operations  22 us (5%)
  blocking collectives  11.7 us (2%)
    psum x2, waiting for transfers between devices, on_device(): multipliers = lax.psum(partial_value, 'col')  220 us
    dot_general x6, matrix products, product(): jnp.dot(first, second, precision=lax.Precision.HIGHEST, preferred_element...  170 us
    another operation x2, local copies, waits for them, and re-layouts  23.5 us
    all_gather x2, waiting for transfers between devices, on_device(): lax.all_gather(rhs_piece, 'row', axis=0, tiled=True)  12.8 us
    psum x1, blocking collectives, on_device(): totals = lax.psum(jnp.sum(right_sides * right_sides, axis=0), 'row')  11.7 us
  transfers between devices with their start and end apart: 6, of which 3 were waited for; matrix products, arithmetic and copies ran while one was open for 31% of the time, Pallas kernels for 0%

commit v1 on v0

v1 whole, which is shorter than its diff:
```python
import functools

import jax
import jax.numpy as jnp
from jax import lax
from jax.experimental import pallas as pl
from jax.experimental.pallas import tpu as pltpu
from jax.sharding import PartitionSpec as P

LANES = 128
F32 = jnp.float32
BF16 = jnp.bfloat16


def split(values):
    high = values.astype(BF16)
    return high, (values - high.astype(F32)).astype(BF16)


def dot(first, second):
    return jnp.dot(first, second, preferred_element_type=F32)


def dot3(first, second):
    (fh, fl), (sh, sl) = first, second
    return dot(fh, sh) + dot(fh, sl) + dot(fl, sh)


def dot2(first, second):
    fh, fl = first
    return dot(fh, second) + dot(fl, second)


def factors_tile(ca, cb, row_block, a, b, inv_a, inv_b, w_ab, pivot_rows):
    in_a, in_b = row_block == a, row_block == b
    m_a = dot2(split(ca), inv_a)
    new_b = cb - dot3(split(m_a), w_ab)
    m_b = dot2(split(new_b), inv_b)
    left_a = m_a - dot3(split(m_b), pivot_rows)
    left_a = jnp.where(in_a, 0.0, jnp.where(in_b, m_a, left_a))
    left_b = jnp.where(in_a | in_b, 0.0, m_b)
    return m_a, new_b, m_b, left_a, left_b


def factors_kernel(
    n_blocks, block, first_row, n_kept, scalars, *refs
):
    ca_refs, cb_refs = refs[:n_blocks], refs[n_blocks : 2 * n_blocks]
    inv_a, inv_b, w_ab, w_ba = refs[2 * n_blocks : 2 * n_blocks + 4]
    out = refs[2 * n_blocks + 4 + n_kept :]
    high_ref, low_ref, fa_ref, fb_ref, wh, wl, ph, pll, ma_s, nb_s, mb_s = out
    a, b, own = scalars[0], scalars[1], scalars[2]

    @pl.when(pl.program_id(0) == 0)
    def _():
        wh[...], wl[...] = split(w_ab[...])
        ph[...], pll[...] = split(dot2(split(w_ba[...]), inv_a[...]))

    rows = high_ref.shape[0]
    start = first_row + pl.program_id(0) * rows
    row_block = (start + lax.broadcasted_iota(jnp.int32, (rows, 1), 0)) // block
    ca = jnp.concatenate([r[...] for r in ca_refs], axis=1)
    cb = jnp.concatenate([r[...] for r in cb_refs], axis=1)
    m_a, new_b, m_b, left_a, left_b = factors_tile(
        ca, cb, row_block, a, b, inv_a[...], inv_b[...],
        (wh[...], wl[...]), (ph[...], pll[...]),
    )
    for left, shift in ((left_a, 0), (left_b, 1)):
        high, low = split(left)
        for r in range(n_blocks):
            there = pl.ds((2 * r + shift) * block, block)
            high_ref[:, there] = high[:, r * block : (r + 1) * block]
            low_ref[:, there] = low[:, r * block : (r + 1) * block]
    ma_s[...], mb_s[...] = m_a, m_b
    mine = pl.ds(pl.multiple_of(own * block, block), block)
    in_a, in_b = row_block == a, row_block == b
    fa_ref[...] = jnp.where(in_a, ca_refs[0][...], ma_s[:, mine]).astype(BF16)
    fb_ref[...] = jnp.where(
        in_a, cb_refs[0][...], jnp.where(in_b, new_b[:, :block], mb_s[:, mine])
    ).astype(BF16)


def factors(ca, cb, inv_a, inv_b, w_ab, w_ba, scalars, row_len, first_row, kept):
    n_blocks, (rows, block) = len(ca), ca[0].shape
    width = n_blocks * block
    tile = tile_of(rows, 384, block)
    first = first_row // tile
    slab = pl.BlockSpec((tile, block), lambda i, s: (i, 0))
    whole = pl.BlockSpec((width, width), lambda i, s: (0, 0))
    shapes = (
        jax.ShapeDtypeStruct((row_len, 2 * width), BF16),
        jax.ShapeDtypeStruct((row_len, 2 * width), BF16),
        jax.ShapeDtypeStruct((row_len, block), BF16),
        jax.ShapeDtypeStruct((row_len, block), BF16),
    )
    n_in = 1 + 2 * n_blocks + 4
    return pl.pallas_call(
        functools.partial(factors_kernel, n_blocks, block, first_row, len(kept)),
        grid_spec=pltpu.PrefetchScalarGridSpec(
            num_scalar_prefetch=1,
            grid=(rows // tile,),
            in_specs=[slab] * (2 * n_blocks)
            + [whole] * 4
            + [pl.BlockSpec(memory_space=pl.ANY)] * len(kept),
            out_specs=[
                pl.BlockSpec((tile, s.shape[1]), lambda i, s: (first + i, 0))
                for s in shapes
            ],
            scratch_shapes=[pltpu.VMEM((width, width), BF16)] * 4
            + [pltpu.VMEM((tile, width), F32)] * 3,
        ),
        out_shape=shapes,
        input_output_aliases={n_in + i: i for i in range(len(kept))},
        name="factors",
    )(scalars, *ca, *cb, inv_a, inv_b, w_ab, w_ba, *kept)


def tile_of(size, most, unit):
    for count in range(1, size // unit + 1):
        if size % (count * unit) == 0 and size // count <= most:
            return size // count
    return unit


def matrix_kernel(block, first_tile, n_kept, scalars, a_ref, high, low, upper, fa, fb, *refs):
    out_ref, uh, ul = refs[n_kept:]

    @pl.when(pl.program_id(1) == 0)
    def _():
        uh[...], ul[...] = split(upper[...])

    update = dot3((high[...], low[...]), (uh[...], ul[...]))
    out_ref[...] = (a_ref[...] - update).astype(BF16)
    width = out_ref.shape[1]
    left_edge = (first_tile + pl.program_id(0)) * width
    for slot, final in ((0, fa), (1, fb)):
        offset = scalars[3 + slot] - left_edge

        @pl.when((scalars[5 + slot] > 0) & (offset >= 0) & (offset < width))
        def _(final=final, offset=offset):
            out_ref[:, pl.ds(pl.multiple_of(offset, block), block)] = final[...]


def update_matrix(matrix, high, low, upper, fa, fb, scalars, first_col, block, tn, kept):
    rows, cols = matrix.shape
    depth, width = upper.shape
    tm = tile_of(rows, 384, block)
    first = first_col // tn
    here = pl.BlockSpec((tm, tn), lambda j, i, s: (i, first + j))
    left = pl.BlockSpec((tm, depth), lambda j, i, s: (i, 0))
    final = pl.BlockSpec((tm, block), lambda j, i, s: (i, 0))
    return pl.pallas_call(
        functools.partial(matrix_kernel, block, first, len(kept)),
        grid_spec=pltpu.PrefetchScalarGridSpec(
            num_scalar_prefetch=1,
            grid=(width // tn, rows // tm),
            in_specs=[
                here, left, left,
                pl.BlockSpec((depth, tn), lambda j, i, s: (0, j)),
                final, final,
            ]
            + [pl.BlockSpec(memory_space=pl.ANY)] * len(kept),
            out_specs=here,
            scratch_shapes=[pltpu.VMEM((depth, tn), BF16)] * 2,
        ),
        out_shape=jax.ShapeDtypeStruct((rows, cols), BF16),
        input_output_aliases={7: 0} if kept else {},
        name="update_matrix",
    )(scalars, matrix, high, low, upper, fa, fb, *kept)


def rhs_kernel(r_ref, high, low, upper, out_ref, sums_ref, uh, ul):
    @pl.when(pl.program_id(0) == 0)
    def _():
        uh[...], ul[...] = split(upper[...])
        sums_ref[...] = jnp.zeros_like(sums_ref)

    new = r_ref[...] - dot3((high[...], low[...]), (uh[...], ul[...]))
    out_ref[...] = new
    sums_ref[...] += jnp.sum(new * new, axis=0, keepdims=True)


def update_rhs(rhs, high, low, upper, block):
    rows, cols = rhs.shape
    depth = upper.shape[0]
    tm = tile_of(rows, 384, block)
    here = pl.BlockSpec((tm, cols), lambda i: (i, 0))
    left = pl.BlockSpec((tm, depth), lambda i: (i, 0))
    return pl.pallas_call(
        rhs_kernel,
        grid=(rows // tm,),
        in_specs=[here, left, left, pl.BlockSpec((depth, cols), lambda i: (0, 0))],
        out_specs=[here, pl.BlockSpec((1, cols), lambda i: (0, 0))],
        out_shape=[
            jax.ShapeDtypeStruct(rhs.shape, F32),
            jax.ShapeDtypeStruct((1, cols), F32),
        ],
        scratch_shapes=[pltpu.VMEM((depth, cols), BF16)] * 2,
        name="update_rhs",
    )(rhs, high, low, upper)


def on_device(matrix, rhs, pivot_inverses, panel_order):
    row_count, col_count = lax.axis_size("row"), lax.axis_size("col")
    width = pivot_inverses.shape[1]
    block = width // row_count
    groups = col_count // row_count
    row_len, col_len = matrix.shape
    total_rows = row_len * row_count
    rhs_len = rhs.shape[1]
    col_index = lax.axis_index("col")
    own, group = col_index % row_count, col_index // row_count
    a, b = panel_order[0], panel_order[1]
    owns = [group == p % groups for p in (a, b)]
    offsets = [p // groups * block for p in (a, b)]
    masks = [0]
    bits = [row_count >> (k + 1) for k in range(row_count.bit_length() - 1)]
    for bit in bits:
        masks = masks + [m ^ bit for m in masks]

    def from_owner(piece, panel):
        chosen = piece
        for step in range(1, groups):
            moved = lax.ppermute(
                piece, "col",
                [(i, (i + step * row_count) % col_count) for i in range(col_count)],
            )
            chosen = jnp.where((group - step) % groups == panel % groups, moved, chosen)
        return chosen

    def spread(piece):
        pieces = [piece]
        for bit in bits:
            swap = [(i, i ^ bit) for i in range(col_count)]
            pieces = pieces + [lax.ppermute(p, "col", swap) for p in pieces]
        return pieces

    panel_rows = [lax.dynamic_slice_in_dim(matrix, p * block, block, 0) for p in (a, b)]
    rhs_rows = [lax.dynamic_slice_in_dim(rhs, p * block, block, 0) for p in (a, b)]
    cross = [
        lax.dynamic_slice_in_dim(panel_rows[0], offsets[1], block, 1),
        lax.dynamic_slice_in_dim(panel_rows[1], offsets[0], block, 1),
    ]
    gather = functools.partial(lax.all_gather, axis_name="row", axis=0, tiled=True)
    head = gather(
        jnp.concatenate(
            [jnp.concatenate([r, c], axis=1) for r, c in zip(rhs_rows, cross)], axis=0
        )
    )
    aligned = block % LANES == 0 and col_len % LANES == 0 and rhs_len % LANES == 0
    tn = tile_of(col_len, 640, block) if aligned else col_len
    n_tiles = col_len // tn
    cut = (n_tiles + 1) // 2 * tn
    both = jnp.concatenate(panel_rows, axis=0)
    uppers = [gather(both[:, :cut])]
    if cut < col_len:
        uppers.append(gather(both[:, cut:]))
    rhs_upper, crossing = head[:, :rhs_len], head[:, rhs_len:]

    halves = 2 if row_len % (2 * block) == 0 else 1
    part = row_len // halves
    slabs = []
    for h in range(halves):
        for p, offset in zip((a, b), offsets):
            piece = lax.dynamic_slice(matrix, (h * part, offset), (part, block))
            slabs.append(spread(from_owner(piece, p)))
    crossing = crossing.reshape(row_count, 2, block, block)
    w_ab = from_owner(crossing[:, 0].reshape(width, block), b)
    w_ba = from_owner(crossing[:, 1].reshape(width, block), a)
    pieces = spread(jnp.concatenate([w_ab, w_ba], axis=0))
    w_ab = jnp.concatenate([p[:width] for p in pieces], axis=1)
    w_ba = jnp.concatenate([p[width:] for p in pieces], axis=1)
    inverses = [
        jnp.concatenate(
            [
                lax.dynamic_slice_in_dim(pivot_inverses[s], (own ^ m) * block, block, 0)
                for m in masks
            ],
            axis=0,
        )
        for s in range(2)
    ]

    if aligned:
        scalars = jnp.stack(
            [a, b, own, offsets[0], offsets[1]] + [o.astype(jnp.int32) for o in owns]
        ).astype(jnp.int32)
        kept = ()
        for h in range(halves):
            kept = factors(
                slabs[2 * h], slabs[2 * h + 1], *inverses, w_ab, w_ba,
                scalars, row_len, h * part, kept,
            )
        high, low, fa, fb = kept
        new_rhs, sums = update_rhs(rhs, high, low, rhs_upper, block)
        out = ()
        for k, upper in enumerate(uppers):
            out = (
                update_matrix(
                    matrix, high, low, upper, fa, fb, scalars, k * cut, block, tn, out
                ),
            )
        factored, sums = out[0], sums[0]
    else:
        row_block = (jnp.arange(row_len, dtype=jnp.int32) // block)[:, None]
        ca, cb = [
            jnp.concatenate(
                [jnp.concatenate(slabs[2 * h + s], axis=1) for h in range(halves)], axis=0
            )
            for s in range(2)
        ]
        m_a, new_b, m_b, left_a, left_b = factors_tile(
            ca, cb, row_block, a, b, *inverses, split(w_ab),
            split(dot2(split(w_ba), inverses[0])),
        )
        left = split(
            jnp.stack(
                [x.reshape(row_len, row_count, block) for x in (left_a, left_b)], axis=2
            ).reshape(row_len, 2 * width)
        )
        new_rhs = rhs - dot3(left, split(rhs_upper))
        sums = jnp.sum(new_rhs * new_rhs, axis=0)
        current = matrix - dot3(left, split(jnp.concatenate(uppers, axis=1)))
        in_a, in_b = row_block == a, row_block == b
        mine = [
            lax.dynamic_slice_in_dim(m, own * block, block, 1) for m in (m_a, m_b)
        ]
        final = (
            jnp.where(in_a, ca[:, :block], mine[0]),
            jnp.where(in_a, cb[:, :block], jnp.where(in_b, new_b[:, :block], mine[1])),
        )
        for values, offset, is_owner in zip(final, offsets, owns):
            old = lax.dynamic_slice_in_dim(current, offset, block, 1)
            current = lax.dynamic_update_slice_in_dim(
                current, jnp.where(is_owner, values, old), offset, 1
            )
        factored = current.astype(BF16)
    totals = lax.psum(sums, "row")
    rhs_norms = jnp.sqrt(totals / total_rows + 1e-06)
    return factored, new_rhs, rhs_norms


def solution(mesh):
    in_specs = (P("row", "col"), P("row", "col"), P(), P())
    out_specs = (P("row", "col"), P("row", "col"), P("col"))
    return jax.shard_map(
        on_device, mesh=mesh, in_specs=in_specs, out_specs=out_specs, check_vma=False
    )
```

time: 485 us -> 335 us (0.69)
  matrix products: 170 us -> 0 us
  Pallas kernels: 0 us -> 131 us
  waiting for transfers between devices: 233 us -> 119 us
  local copies, waits for them, and re-layouts: 42.5 us -> 17.3 us
  starting transfers between devices: 0.65 us -> 18.5 us
  other arithmetic: 4.62 us -> 14.8 us
    psum x2 -> x0, waiting for transfers between devices: 220 us -> none  [on_device(): multipliers = lax.psum(partial_value, 'col')]
    dot_general x6 -> x0, matrix products: 170 us -> none  [product(): jnp.dot(first, second, precision=lax.Precision.HIGHEST, preferred_element...]
    pallas_call x0 -> x5, Pallas kernels: none -> 131 us  [the longest x2 72.5 us: update_matrix(): pl.pallas_call(functools.partial(matrix_kernel, block, first, len(kept)),...]
    ppermute x0 -> x21, waiting for transfers between devices: none -> 119 us  [the longest x6 76.7 us: from_owner(): lax.ppermute(piece, 'col', [(i, (i + step * row_count) % col_count) for i...]
    another operation x2 -> x1, local copies, waits for them, and re-layouts: 23.5 us -> 0.66 us  [on_device(): jnp.stack([a, b, own, offsets[0], offsets[1]] + [o.astype(jnp.int32) for...]
    ppermute x0 -> x21, starting transfers between devices: none -> 18.3 us  [the longest x15 9.69 us: spread(): pieces = pieces + [lax.ppermute(p, 'col', swap) for p in pieces]]
    all_gather x4 -> x3, waiting for transfers between devices: 12.8 us -> 0.01 us  [the longest x1 0.01 us: on_device(): gather(jnp.concatenate([jnp.concatenate([r, c], axis=1) for r, c in zip(r...]
    select_n x0 -> x6, other arithmetic: none -> 7.24 us  [from_owner(): chosen = jnp.where((group - step) % groups == panel % groups, moved, chosen)]
  transfers between devices with their start and end apart: 6 -> 24, of which waited for: 3 -> 9; matrix products, arithmetic and copies ran while one was open for 31% -> 8% of each run, Pallas kernels for 0% -> 32%
where the time goes in v1:
time: 335 us; the launch traced here: 334 us
  Pallas kernels  131 us (39%)
  waiting for transfers between devices  119 us (36%)
  between operations  20.5 us (6%)
  starting transfers between devices  18.5 us (6%)
  local copies, waits for them, and re-layouts  17.3 us (5%)
  other arithmetic  14.8 us (4%)
  blocking collectives  12.2 us (4%)
    ppermute x6, waiting for transfers between devices, from_owner(): lax.ppermute(piece, 'col', [(i, (i + step * row_count) % col_count) for i...  76.7 us
    pallas_call x2, Pallas kernels, update_matrix(): pl.pallas_call(functools.partial(matrix_kernel, block, first, len(kept)),...  72.5 us
    ppermute x15, waiting for transfers between devices, spread(): pieces = pieces + [lax.ppermute(p, 'col', swap) for p in pieces]  42.7 us
    pallas_call x2, Pallas kernels, factors(): pl.pallas_call(functools.partial(factors_kernel, n_blocks, block, first_r...  38.2 us
    pallas_call x1, Pallas kernels, update_rhs(): pl.pallas_call(rhs_kernel, grid=(rows // tm,), in_specs=[here, left, left...  20.3 us
    psum x1, blocking collectives, on_device(): totals = lax.psum(sums, 'row')  12.2 us
    ppermute x15, starting transfers between devices, spread(): pieces = pieces + [lax.ppermute(p, 'col', swap) for p in pieces]  9.69 us
    ppermute x6, starting transfers between devices, from_owner(): lax.ppermute(piece, 'col', [(i, (i + step * row_count) % col_count) for i...  8.65 us
  transfers between devices with their start and end apart: 24, of which 9 were waited for; matrix products, arithmetic and copies ran while one was open for 8% of the time, Pallas kernels for 32%

profile of v1, /device:TPU:0, one launch (start us, length us, event | category | flops | bytes accessed | tf_op | source)
XLA Modules:
  0.0 333.7 jit_solution(14360850576363640879)
XLA Ops:
  7.2 1.3 fusion.6
  18.1 1.6 constant_dynamic-slice_fusion.1
  21.1 3.8 %constant_dynamic-slice_fusion.2 = (f32[1920,128]{1,0:T(8,128)S(1)}, f32[1920,128]{1,0:T(8,128)}, f32[1920,128]{1,0:T(8,128)}, f32[1920,128]{1,0:T(8,128)}) fusion(f32[3840,1920]{1,0:T(8,128)} %a_ref.3, s32[]{:T(128)S(6)} %select_n.140, s32[]{:T(128)S(6)} %select_n.137), kind=kLoop, calls=%fused_computation.24 | loop fusion | bytes 7864328 | tf_op jit(solution)/shard_map/dynamic_slice | solution.py:265
  24.9 3.0 collective-permute-start
  28.0 2.0 collective-permute-start.13
  31.0 19.9 %collective-permute-done = f32[1920,128]{1,0:T(8,128)} collective-permute-done((f32[1920,128]{1,0:T(8,128)}, f32[1920,128]{1,0:T(8,128)}, u32[]{:S(2)}, u32[]{:S(2)}) %collective-permute-start) | collective-permute-done | bytes 983072 | tf_op jit(solution)/shard_map/ppermute | solution.py:224
  50.8 2.3 broadcast_select_fusion.3.refs_0_
  53.1 2.0 collective-permute-start.1
  55.1 16.8 %collective-permute-done.4 = f32[1920,128]{1,0:T(8,128)} collective-permute-done((f32[1920,128]{1,0:T(8,128)}, f32[1920,128]{1,0:T(8,128)}, u32[]{:S(2)}, u32[]{:S(2)}) %collective-permute-start.4) | collective-permute-done | bytes 983072 | tf_op jit(solution)/shard_map/ppermute | solution.py:224
  71.9 2.3 broadcast_select_fusion.1.refs_4_
  74.2 2.0 collective-permute-start.5
  77.3 1.6 collective-permute-start.9
  78.9 14.1 %collective-permute-done.13 = f32[1920,128]{1,0:T(8,128)} collective-permute-done((f32[1920,128]{1,0:T(8,128)}, f32[1920,128]{1,0:T(8,128)}, u32[]{:S(2)}, u32[]{:S(2)}) %collective-permute-start.13) | collective-permute-done | bytes 983072 | tf_op jit(solution)/shard_map/ppermute | solution.py:224
  93.0 2.0 collective-permute-start.8
  95.0 1.3 broadcast_select_fusion.2.refs_0_
  96.3 23.2 %collective-permute-done.9 = f32[512,128]{1,0:T(8,128)S(1)} collective-permute-done((f32[512,128]{1,0:T(8,128)S(1)}, f32[512,128]{1,0:T(8,128)S(1)}, u32[]{:S(2)}, u32[]{:S(2)}) %collective-permute-start.9) | collective-permute-done | bytes 262176 | tf_op jit(solution)/shard_map/ppermute | solution.py:224
  119.6 2.0 collective-permute-start.14
  121.6 2.7 collective-permute-done.8
  125.2 1.7 collective-permute-start.10
  126.9 1.3 broadcast_select_fusion.refs_4_
  128.6 15.7 %collective-permute-done.14.refs_1_ = f32[1920,128]{1,0:T(8,128)} collective-permute-done((f32[1920,128]{1,0:T(8,128)S(1)}, f32[1920,128]{1,0:T(8,128)}, u32[]{:S(2)}, u32[]{:S(2)}) %collective-permute-start.14) | collective-permute-done | bytes 983072 | tf_op jit(solution)/shard_map/ppermute | solution.py:235
  145.5 10.1 %collective-permute-done.10 = f32[1024,128]{1,0:T(8,128)} collective-permute-done((f32[1024,128]{1,0:T(8,128)}, f32[1024,128]{1,0:T(8,128)}, u32[]{:S(2)}, u32[]{:S(2)}) %collective-permute-start.10) | collective-permute-done | bytes 524320 | tf_op jit(solution)/shard_map/ppermute | solution.py:235
  155.5 1.3 fusion.1
  157.8 16.3 %collective-permute-done.18.refs_5_ = f32[1920,128]{1,0:T(8,128)S(1)} collective-permute-done((f32[1920,128]{1,0:T(8,128)S(1)}, f32[1920,128]{1,0:T(8,128)S(1)}, u32[]{:S(2)}, u32[]{:S(2)}) %collective-permute-start.18) | collective-permute-done | bytes 983072 | tf_op jit(solution)/shard_map/ppermute | solution.py:235
  175.9 3.1 slice.80.upper
  180.2 1.6 pad_maximum_fusion.1
  183.4 19.1 %factors.2 = (bf16[3840,1024]{1,0:T(8,128)(2,1)}, bf16[3840,1024]{1,0:T(8,128)(2,1)}, bf16[3840,128]{1,0:T(8,128)(2,1)}, bf16[3840,128]{1,0:T(8,128)(2,1)}) custom-call(s32[7]{0:T(128)} %stack.31.scalars, f32[1920,128]{1,0:T(8,128)} %copy-done, f32[1920,128]{1,0:T(8,128)} %collective-permute-done.14.refs_1_, f32[1920,128]{1,0:T(8,128)} %collective-permute-done.15.refs_2_, ...), custom_call_target="tpu_custom_call" | custom-call | tf_op jit(solution)/shard_map/factors/pallas_call | solution.py:97
  202.5 19.1 %factors.3 = (bf16[3840,1024]{1,0:T(8,128)(2,1)}, bf16[3840,1024]{1,0:T(8,128)(2,1)}, bf16[3840,128]{1,0:T(8,128)(2,1)}, bf16[3840,128]{1,0:T(8,128)(2,1)}) custom-call(s32[7]{0:T(128)} %stack.31.scalars, f32[1920,128]{1,0:T(8,128)} %broadcast_select_fusion.3.refs_0_, ...), custom_call_target="tpu_custom_call", output_to_operand_aliasing={{0}: (13, {}), {1}: (14, {}), {2}: (15, {}), {3}: (16, {})} | custom-call | tf_op jit(solution)/shard_map/factors/pallas_call | solution.py:97
  221.6 20.3 %update_rhs.1 = (f32[3840,512]{1,0:T(8,128)}, f32[1,512]{1,0:T(1,128)}) custom-call(f32[3840,512]{1,0:T(8,128)} %r_ref.1, bf16[3840,1024]{1,0:T(8,128)(2,1)} %get-tuple-element.17.high, bf16[3840,1024]{1,0:T(8,128)(2,1)} %get-tuple-element.18.low, f32[1024,512]{1,0:T(8,128)} %slice.80.upper), custom_call_target="tpu_custom_call" | custom-call | tf_op jit(solution)/shard_map/update_rhs/pallas_call | solution.py:189
  241.9 12.2 %psum.7 = f32[512]{0:T(512)S(1)} all-reduce(f32[512]{0:T(512)} %bitcast.32), channel_id=1, replica_groups=mesh['row'=4,'col'=8] {'row'}, use_global_device_ids=true, to_apply=%region_0.1 | all-reduce | flops 512 | bytes 4096 | tf_op jit(solution)/shard_map/psum | solution.py:338
  254.7 46.9 %update_matrix.2.refs_0_ = bf16[3840,1920]{1,0:T(8,128)(2,1)} custom-call(s32[7]{0:T(128)} %stack.31.scalars, f32[3840,1920]{1,0:T(8,128)} %a_ref.3, bf16[3840,1024]{1,0:T(8,128)(2,1)} %get-tuple-element.17.high, bf16[3840,1024]{1,0:T(8,128)(2,1)} %get-tuple-element.18.low, f32[1024,1280]{1,0:T(8,128)} %all-gather.8.cloned.1.call-done.upper, ...), custom_call_target="tpu_custom_call" | custom-call | tf_op jit(solution)/shard_map/update_matrix/pallas_call | solution.py:152
  301.6 25.6 %update_matrix.3 = bf16[3840,1920]{1,0:T(8,128)(2,1)} custom-call(s32[7]{0:T(128)} %stack.31.scalars, f32[3840,1920]{1,0:T(8,128)} %a_ref.3, bf16[3840,1024]{1,0:T(8,128)(2,1)} %get-tuple-element.17.high, bf16[3840,1024]{1,0:T(8,128)(2,1)} %get-tuple-element.18.low, f32[1024,640]{1,0:T(8,128)} %all-gather.6.cloned.1.call-done.upper, ...), custom_call_target="tpu_custom_call", output_to_operand_aliasing={{}: (7, {})} | custom-call | tf_op jit(solution)/shard_map/update_matrix/pallas_call | solution.py:152
  (63 shorter events, 15.2 us)
Async XLA Ops:
  7.2 69.0 %all-gather.4.cloned.1.call-start = ((), (), s32[]{:S(2)}) async-start(), calls=%async_computation | async-start | bytes 3276800 | tf_op jit(solution)/shard_map/all_gather | solution.py:245
  18.1 236.6 %all-gather.8.cloned.1.call-start = ((), (), s32[]{:S(2)}) async-start(), calls=%async_computation.2 | async-start | bytes 6553600 | tf_op jit(solution)/shard_map/all_gather | solution.py:255
  21.0 280.6 %all-gather.6.cloned.1.call-start = ((), (), s32[]{:S(2)}) async-start(), calls=%async_computation.1 | async-start | bytes 3276800 | tf_op jit(solution)/shard_map/all_gather | solution.py:257
  24.9 25.9 %collective-permute-start = (f32[1920,128]{1,0:T(8,128)}, f32[1920,128]{1,0:T(8,128)}, u32[]{:S(2)}, u32[]{:S(2)}) collective-permute-start(f32[1920,128]{1,0:T(8,128)} %get-tuple-element.28), channel_id=1, source_target_pairs={{0,4},{1,5},{2,6},{3,7},{4,0},{5,1},{6,2},{7,3},{8,12},{9,13},{10,... | collective-permute-start | bytes 2949128 | tf_op jit(solution)/shard_map/ppermute | solution.py:224
  27.9 44.0 %collective-permute-start.4 = (f32[1920,128]{1,0:T(8,128)}, f32[1920,128]{1,0:T(8,128)}, u32[]{:S(2)}, u32[]{:S(2)}) collective-permute-start(f32[1920,128]{1,0:T(8,128)} %get-tuple-element.27), channel_id=1, source_target_pairs={{0,4},{1,5},{2,6},{3,7},{4,0},{5,1},{6,2},{7,3},{8,12},{9,13},{10,... | collective-permute-start | bytes 2949128 | tf_op jit(solution)/shard_map/ppermute | solution.py:224
  28.0 65.0 %collective-permute-start.13 = (f32[1920,128]{1,0:T(8,128)}, f32[1920,128]{1,0:T(8,128)}, u32[]{:S(2)}, u32[]{:S(2)}) collective-permute-start(f32[1920,128]{1,0:T(8,128)} %get-tuple-element.26), channel_id=1, source_target_pairs={{0,4},{1,5},{2,6},{3,7},{4,0},{5,1},{6,2},{7,3},{8,12},{9,13},{10,... | collective-permute-start | bytes 2949128 | tf_op jit(solution)/shard_map/ppermute | solution.py:224
  30.0 95.2 %collective-permute-start.17 = (f32[1920,128]{1,0:T(8,128)S(1)}, f32[1920,128]{1,0:T(8,128)}, u32[]{:S(2)}, u32[]{:S(2)}) collective-permute-start(f32[1920,128]{1,0:T(8,128)S(1)} %get-tuple-element.25), channel_id=1, source_target_pairs={{0,4},{1,5},{2,6},{3,7},{4,0},{5,1},{6,2},{7,3},{8,12},{9,13},{10,... | collective-permute-start | bytes 2949128 | tf_op jit(solution)/shard_map/ppermute | solution.py:224
  30.9 113.4 %copy-start.4 = (s32[2]{0:T(128)S(1)}, s32[2]{0:T(128)}, u32[]{:S(2)}) copy-start(s32[2]{0:T(128)} %param.7) | copy-start | bytes 28
  53.1 75.1 %collective-permute-start.1 = (f32[1920,128]{1,0:T(8,128)}, f32[1920,128]{1,0:T(8,128)}, u32[]{:S(2)}, u32[]{:S(2)}) collective-permute-start(f32[1920,128]{1,0:T(8,128)} %broadcast_select_fusion.3.refs_0_), channel_id=1, source_target_pairs={{0,2},{1,3},{2,0},{3,1},{4,6},{5,7},{6,4},{7,5},{8,10},{9,11},{10,... | collective-permute-start | bytes 2949128 | tf_op jit(solution)/shard_map/ppermute | solution.py:235
  74.2 54.4 %collective-permute-start.5 = (f32[1920,128]{1,0:T(8,128)}, f32[1920,128]{1,0:T(8,128)}, u32[]{:S(2)}, u32[]{:S(2)}) collective-permute-start(f32[1920,128]{1,0:T(8,128)} %broadcast_select_fusion.1.refs_4_), channel_id=1, source_target_pairs={{0,2},{1,3},{2,0},{3,1},{4,6},{5,7},{6,4},{7,5},{8,10},{9,11},{10,... | collective-permute-start | bytes 2949128 | tf_op jit(solution)/shard_map/ppermute | solution.py:235
  77.3 42.2 %collective-permute-start.9 = (f32[512,128]{1,0:T(8,128)S(1)}, f32[512,128]{1,0:T(8,128)S(1)}, u32[]{:S(2)}, u32[]{:S(2)}) collective-permute-start(f32[512,128]{1,0:T(8,128)S(1)} %bitcast.31), channel_id=1, source_target_pairs={{0,4},{1,5},{2,6},{3,7},{4,0},{5,1},{6,2},{7,3},{8,12},{9,13},{10,... | collective-permute-start | bytes 786440 | tf_op jit(solution)/shard_map/ppermute | solution.py:224
  93.0 31.3 %collective-permute-start.8 = (f32[512,128]{1,0:T(8,128)S(1)}, f32[512,128]{1,0:T(8,128)S(1)}, u32[]{:S(2)}, u32[]{:S(2)}) collective-permute-start(f32[512,128]{1,0:T(8,128)S(1)} %bitcast.30), channel_id=1, source_target_pairs={{0,4},{1,5},{2,6},{3,7},{4,0},{5,1},{6,2},{7,3},{8,12},{9,13},{10,... | collective-permute-start | bytes 786440 | tf_op jit(solution)/shard_map/ppermute | solution.py:224
  96.3 82.7 %copy-start = (f32[1920,128]{1,0:T(8,128)}, f32[1920,128]{1,0:T(8,128)S(1)}, u32[]{:S(2)}) copy-start(f32[1920,128]{1,0:T(8,128)S(1)} %broadcast_select_fusion.2.refs_0_) | copy-start | bytes 2949124
  119.6 24.7 %collective-permute-start.14 = (f32[1920,128]{1,0:T(8,128)S(1)}, f32[1920,128]{1,0:T(8,128)}, u32[]{:S(2)}, u32[]{:S(2)}) collective-permute-start(f32[1920,128]{1,0:T(8,128)S(1)} %broadcast_select_fusion.2.refs_0_), channel_id=1, source_target_pairs={{0,2},{1,3},{2,0},{3,1},{4,6},{5,7},{6,4},{7,5},{8,10},{9,11},{10,... | collective-permute-start | bytes 2949128 | tf_op jit(solution)/shard_map/ppermute | solution.py:235
  124.3 20.6 %collective-permute-start.15 = (f32[1920,128]{1,0:T(8,128)S(1)}, f32[1920,128]{1,0:T(8,128)}, u32[]{:S(2)}, u32[]{:S(2)}) collective-permute-start(f32[1920,128]{1,0:T(8,128)S(1)} %broadcast_select_fusion.2.refs_0_), channel_id=1, source_target_pairs={{0,1},{1,0},{2,3},{3,2},{4,5},{5,4},{6,7},{7,6},{8,9},{9,8},{10,11... | collective-permute-start | bytes 2949128 | tf_op jit(solution)/shard_map/ppermute | solution.py:235
  125.2 30.3 %collective-permute-start.10 = (f32[1024,128]{1,0:T(8,128)}, f32[1024,128]{1,0:T(8,128)}, u32[]{:S(2)}, u32[]{:S(2)}) collective-permute-start(f32[1024,128]{1,0:T(8,128)} %pad_maximum_fusion.6), channel_id=1, source_target_pairs={{0,2},{1,3},{2,0},{3,1},{4,6},{5,7},{6,4},{7,5},{8,10},{9,11},{10,... | collective-permute-start | bytes 1572872 | tf_op jit(solution)/shard_map/ppermute | solution.py:235
  128.2 53.5 %copy-start.1 = (f32[1920,128]{1,0:T(8,128)}, f32[1920,128]{1,0:T(8,128)S(1)}, u32[]{:S(2)}) copy-start(f32[1920,128]{1,0:T(8,128)S(1)} %broadcast_select_fusion.refs_4_) | copy-start | bytes 2949124
  128.2 45.8 %collective-permute-start.18 = (f32[1920,128]{1,0:T(8,128)S(1)}, f32[1920,128]{1,0:T(8,128)S(1)}, u32[]{:S(2)}, u32[]{:S(2)}) collective-permute-start(f32[1920,128]{1,0:T(8,128)S(1)} %broadcast_select_fusion.refs_4_), channel_id=1, source_target_pairs={{0,2},{1,3},{2,0},{3,1},{4,6},{5,7},{6,4},{7,5},{8,10},{9,11},{10,... | collective-permute-start | bytes 2949128 | tf_op jit(solution)/shard_map/ppermute | solution.py:235
  128.6 45.4 %collective-permute-start.19 = (f32[1920,128]{1,0:T(8,128)S(1)}, f32[1920,128]{1,0:T(8,128)}, u32[]{:S(2)}, u32[]{:S(2)}) collective-permute-start(f32[1920,128]{1,0:T(8,128)S(1)} %broadcast_select_fusion.refs_4_), channel_id=1, source_target_pairs={{0,1},{1,0},{2,3},{3,2},{4,5},{5,4},{6,7},{7,6},{8,9},{9,8},{10,11... | collective-permute-start | bytes 2949128 | tf_op jit(solution)/shard_map/ppermute | solution.py:235
  144.3 30.3 %collective-permute-start.16 = (f32[1920,128]{1,0:T(8,128)}, f32[1920,128]{1,0:T(8,128)}, u32[]{:S(2)}, u32[]{:S(2)}) collective-permute-start(f32[1920,128]{1,0:T(8,128)} %collective-permute-done.14.refs_1_), channel_id=1, source_target_pairs={{0,1},{1,0},{2,3},{3,2},{4,5},{5,4},{6,7},{7,6},{8,9},{9,8},{10,11... | collective-permute-start | bytes 2949128 | tf_op jit(solution)/shard_map/ppermute | solution.py:235
  145.0 29.7 %collective-permute-start.11 = (f32[1024,128]{1,0:T(8,128)}, f32[1024,128]{1,0:T(8,128)S(1)}, u32[]{:S(2)}, u32[]{:S(2)}) collective-permute-start(f32[1024,128]{1,0:T(8,128)} %pad_maximum_fusion.6), channel_id=1, source_target_pairs={{0,1},{1,0},{2,3},{3,2},{4,5},{5,4},{6,7},{7,6},{8,9},{9,8},{10,11... | collective-permute-start | bytes 1572872 | tf_op jit(solution)/shard_map/ppermute | solution.py:235
  155.5 19.5 %collective-permute-start.12 = (f32[1024,128]{1,0:T(8,128)}, f32[1024,128]{1,0:T(8,128)S(1)}, u32[]{:S(2)}, u32[]{:S(2)}) collective-permute-start(f32[1024,128]{1,0:T(8,128)} %collective-permute-done.10), channel_id=1, source_target_pairs={{0,1},{1,0},{2,3},{3,2},{4,5},{5,4},{6,7},{7,6},{8,9},{9,8},{10,11... | collective-permute-start | bytes 1572872 | tf_op jit(solution)/shard_map/ppermute | solution.py:235
  174.0 9.4 %copy-start.2 = (f32[1920,128]{1,0:T(8,128)}, f32[1920,128]{1,0:T(8,128)S(1)}, u32[]{:S(2)}) copy-start(f32[1920,128]{1,0:T(8,128)S(1)} %collective-permute-done.18.refs_5_) | copy-start | bytes 2949124
  174.0 28.4 %collective-permute-start.2 = (f32[1920,128]{1,0:T(8,128)}, f32[1920,128]{1,0:T(8,128)}, u32[]{:S(2)}, u32[]{:S(2)}) collective-permute-start(f32[1920,128]{1,0:T(8,128)} %broadcast_select_fusion.3.refs_0_), channel_id=1, source_target_pairs={{0,1},{1,0},{2,3},{3,2},{4,5},{5,4},{6,7},{7,6},{8,9},{9,8},{10,11... | collective-permute-start | bytes 2949128 | tf_op jit(solution)/shard_map/ppermute | solution.py:235
  174.0 28.5 %collective-permute-start.6 = (f32[1920,128]{1,0:T(8,128)}, f32[1920,128]{1,0:T(8,128)}, u32[]{:S(2)}, u32[]{:S(2)}) collective-permute-start(f32[1920,128]{1,0:T(8,128)} %broadcast_select_fusion.1.refs_4_), channel_id=1, source_target_pairs={{0,1},{1,0},{2,3},{3,2},{4,5},{5,4},{6,7},{7,6},{8,9},{9,8},{10,11... | collective-permute-start | bytes 2949128 | tf_op jit(solution)/shard_map/ppermute | solution.py:235
  174.6 28.0 %collective-permute-start.3 = (f32[1920,128]{1,0:T(8,128)}, f32[1920,128]{1,0:T(8,128)}, u32[]{:S(2)}, u32[]{:S(2)}) collective-permute-start(f32[1920,128]{1,0:T(8,128)} %collective-permute-done.1.refs_1_), channel_id=1, source_target_pairs={{0,1},{1,0},{2,3},{3,2},{4,5},{5,4},{6,7},{7,6},{8,9},{9,8},{10,11... | collective-permute-start | bytes 2949128 | tf_op jit(solution)/shard_map/ppermute | solution.py:235
  174.6 27.9 %collective-permute-start.7 = (f32[1920,128]{1,0:T(8,128)}, f32[1920,128]{1,0:T(8,128)}, u32[]{:S(2)}, u32[]{:S(2)}) collective-permute-start(f32[1920,128]{1,0:T(8,128)} %collective-permute-done.5.refs_5_), channel_id=1, source_target_pairs={{0,1},{1,0},{2,3},{3,2},{4,5},{5,4},{6,7},{7,6},{8,9},{9,8},{10,11... | collective-permute-start | bytes 2949128 | tf_op jit(solution)/shard_map/ppermute | solution.py:235
  175.1 7.4 %collective-permute-start.20 = (f32[1920,128]{1,0:T(8,128)S(1)}, f32[1920,128]{1,0:T(8,128)S(1)}, u32[]{:S(2)}, u32[]{:S(2)}) collective-permute-start(f32[1920,128]{1,0:T(8,128)S(1)} %collective-permute-done.18.refs_5_), channel_id=1, source_target_pairs={{0,1},{1,0},{2,3},{3,2},{4,5},{5,4},{6,7},{7,6},{8,9},{9,8},{10,11... | collective-permute-start | bytes 2949128 | tf_op jit(solution)/shard_map/ppermute | solution.py:235
  182.4 1.0 copy-start.3
Sparse Core Ops, SparseCore 0:
  18.2 57.4 all-gather.3
  77.3 96.7 all-gather.7
  175.7 53.0 all-gather.5
